TPU v7x, 32 devices: a whole 2x2x4 slice. The times are simulated.
32 devices in a mesh: seq: 8 (over z, y), head: 4 (over x, core).
Axes of the slice: x: 2, y: 2, z: 4, core: 2. Of those that a mesh axis runs over, the one named last changes fastest.
Arguments:
- inputs: bfloat16 [2048, 5120], P('seq', 'head'), may hold values from -6 to 6
- time_step: float32 [80, 2048], P('head', 'seq'), may hold values from 0.01 to 0.3
- decay_rate: float32 [80], P('head'), may hold values from 0.0001 to 1
- input_map: bfloat16 [2048, 128], P('seq'), may hold values from -6 to 6
- output_map: bfloat16 [2048, 128], P('seq'), may hold values from -0.59765625 to 0.59765625
- output_grad: bfloat16 [2048, 5120], P('seq', 'head'), may hold values from -3 to 3
- span_states: float32 [8, 80, 64, 128], P('seq', 'head'), may hold values from -6 to 6
- resets: int32 [8], P('seq'), may hold values from 0 to 4095
Outputs:
- grad_inputs: bfloat16 [2048, 5120], P('seq', 'head')
- grad_input_map: float32 [2048, 128], P('seq')
- grad_rate: float32 [80], P('head')
Inputs may be any that keep to these rules, and one draw needn't show every extreme that they name: `resets`: A value p under 256 means that a document starts at position p of that span; a value of 256 or more means that none starts in it.
All inputs are finite; a program needn't handle non-finite values.
Results may differ from a plain program's by a relative error of at most 0.003.
Values sent between devices are 32-bit elements; how exact they have to be, the bound alone decides.
A program may use at most 64 MiB of HBM per device.

v0:
```python
import jax
import jax.numpy as jnp
from jax import lax
from jax.sharding import PartitionSpec as P

highest = lax.Precision.HIGHEST


def prepare(x_block, step_block, decay_rate, b_block, c_block, grad_block, start_state, reset_at):
    block_len = step_block.shape[1]
    positions = jnp.arange(block_len, dtype=jnp.int32)
    later_doc = positions >= reset_at
    no_reset = reset_at >= block_len
    elapsed = jnp.cumsum(step_block, axis=1)
    log_decay = -decay_rate[:, None] * elapsed
    joined = (later_doc[:, None] == later_doc[None, :]) & (positions[None, :] >= positions[:, None])
    log_gaps = log_decay[:, None, :] - log_decay[:, :, None]
    pair_weight = jnp.where(joined[None], jnp.exp(jnp.where(joined[None], log_gaps, 0.0)), 0.0)
    intersection = jnp.dot(b_block, c_block.T, preferred_element_type=jnp.float32)
    products = jnp.einsum("shp,uhp->hsu", x_block, grad_block, preferred_element_type=jnp.float32)
    mixing = (pair_weight * intersection[None]).astype(jnp.bfloat16)
    pair_terms = pair_weight * products
    paired = pair_terms.astype(jnp.bfloat16)
    dx_inner = jnp.einsum("hsu,uhp->shp", mixing, grad_block, preferred_element_type=jnp.float32)
    db_inner = jnp.einsum("hsu,un->hsn", paired, c_block, preferred_element_type=jnp.float32)
    start_weight = jnp.where(later_doc[None], 0.0, jnp.exp(log_decay))
    end_weight = jnp.where(
        (later_doc | no_reset)[None], jnp.exp(log_decay[:, -1:] - log_decay), 0.0
    )
    carry_gain = jnp.where(no_reset, jnp.exp(log_decay[:, -1]), 0.0)
    c_wide = c_block.astype(jnp.float32)
    grad_wide = grad_block.astype(jnp.float32)
    weighted_c = start_weight[:, :, None] * c_wide[None]
    boundary_grad = jnp.einsum("hun,uhp->hpn", weighted_c, grad_wide, precision=highest)
    state_read = jnp.einsum("uhp,hpn->hun", grad_wide, start_state, precision=highest)
    start_term = jnp.sum(state_read * c_wide[None], axis=2)
    inside_term = jnp.sum(
        pair_terms
        * intersection[None]
        * step_block[:, :, None]
        * (elapsed[:, None, :] - elapsed[:, :, None]),
        axis=(1, 2),
    )
    entry_term = jnp.sum(start_weight * elapsed * start_term, axis=1)
    return (
        carry_gain,
        boundary_grad,
        dx_inner,
        db_inner,
        inside_term + entry_term,
        end_weight,
        elapsed,
    )


def finish(prepared, x_block, step_block, b_block, start_state, carried):
    carry_gain, boundary_grad, dx_inner, db_inner, partial_rate, end_weight, elapsed = prepared
    b_wide = b_block.astype(jnp.float32)
    x_wide = x_block.astype(jnp.float32)
    carried_b = jnp.einsum("sn,hpn->shp", b_wide, carried, precision=highest)
    carried_x = jnp.einsum("shp,hpn->hsn", x_wide, carried, precision=highest)
    step_rows = step_block.T[:, :, None]
    end_rows = end_weight.T[:, :, None]
    grad_x = (step_rows * (dx_inner + end_rows * carried_b)).astype(jnp.bfloat16)
    grad_b = jnp.sum(
        step_block[:, :, None] * (db_inner + end_weight[:, :, None] * carried_x), axis=0
    )
    last_elapsed = elapsed[:, -1]
    leaving_term = jnp.sum(
        end_weight
        * step_block
        * (last_elapsed[:, None] - elapsed)
        * jnp.sum(carried_x * b_wide[None], axis=2),
        axis=1,
    )
    through_term = carry_gain * last_elapsed * jnp.sum(carried * start_state, axis=(1, 2))
    return (grad_x, grad_b, partial_rate + leaving_term + through_term)


def backward_step(running, members):
    grad_piece, gain_piece = members
    return (grad_piece + gain_piece[:, None] * running, running)


def body(inputs, time_step, decay_rate, input_map, output_map, output_grad, span_states, resets):
    length = time_step.shape[1]
    block_count = span_states.shape[0]
    block_len = length // block_count
    head_count = decay_rate.shape[0]
    head_width = inputs.shape[1] // head_count
    number = 0
    x_block = inputs.reshape(block_len, head_count, head_width)
    grad_block = output_grad.reshape(block_len, head_count, head_width)
    step_block = time_step
    b_block = input_map
    prepared = prepare(
        x_block,
        step_block,
        decay_rate,
        b_block,
        output_map,
        grad_block,
        span_states[number],
        resets[number],
    )
    pieces = [(prepared, x_block, step_block, b_block)]
    gain_total = jnp.ones((head_count,), jnp.float32)
    grad_total = jnp.zeros_like(span_states[0])
    for number in reversed(range(block_count)):
        gain_block, grad_block_sum = (pieces[number][0][0], pieces[number][0][1])
        grad_total = grad_block_sum + gain_block[:, None, None] * grad_total
        gain_total = gain_block * gain_total
    seq_count = lax.axis_size("seq")
    entries = grad_total.shape[1] * grad_total.shape[2]
    sliced = grad_total.reshape(head_count, seq_count, entries // seq_count)
    received = lax.all_to_all(sliced, "seq", split_axis=1, concat_axis=1, tiled=True)
    gains = lax.all_gather(gain_total[None], "seq", axis=0, tiled=True)
    ending, exclusive = lax.scan(
        backward_step,
        jnp.zeros_like(received[:, 0]),
        (jnp.transpose(received, (1, 0, 2)), gains),
        reverse=True,
    )
    returned = lax.all_to_all(
        jnp.transpose(exclusive, (1, 0, 2)), "seq", split_axis=1, concat_axis=1, tiled=True
    )
    incoming = returned.reshape(grad_total.shape)
    carried = incoming
    grad_x_list = [None] * block_count
    grad_b_list = [None] * block_count
    rate_total = jnp.zeros((head_count,), jnp.float32)
    for number in reversed(range(block_count)):
        prepared, x_block, step_block, b_block = pieces[number]
        grad_x, grad_b, rate_part = finish(
            prepared, x_block, step_block, b_block, span_states[number], carried
        )
        grad_x_list[number] = grad_x.reshape(block_len, head_count * head_width)
        grad_b_list[number] = grad_b
        rate_total = rate_part
        carried = prepared[1] + prepared[0][:, None, None] * carried
    grad_inputs = grad_x_list[0]
    grad_input_map = lax.psum(grad_b_list[0], "head")
    grad_rate = -lax.psum(rate_total, "seq")
    return (grad_inputs, grad_input_map, grad_rate)


def solution(mesh):
    in_specs = (
        P("seq", "head"),
        P("head", "seq"),
        P("head"),
        P("seq", None),
        P("seq", None),
        P("seq", "head"),
        P("seq", "head", None, None),
        P("seq"),
    )
    out_specs = (P("seq", "head"), P("seq", None), P("head"))
    return jax.shard_map(body, mesh=mesh, in_specs=in_specs, out_specs=out_specs, check_vma=False)
```

profile of v0, /device:TPU:0, one launch (start us, length us, event | category | flops | bytes accessed | tf_op | source)
XLA Modules:
  0.0 141.0 jit_solution(17333116644024165966)
XLA Ops:
  8.6 0.8 reshape.290
  11.2 0.9 copy.37
  12.2 1.4 copy.36
  13.6 1.7 %fusion.31 = f32[20,64,128]{2,1,0:T(8,128)S(1)} fusion(bf16[256,20,64]{0,2,1:T(8,128)(2,1)S(1)} %bitcast.80, f32[256,128]{0,1:T(8,128)S(1)} %copy.37, f32[20,256]{1,0:T(8,128)S(1)} %get-tuple-element.152, f32[20]{0:T(128)S(1)} %broadcast_multiply_fusion.1), kind=kOutput, calls=%fused_computation.38 | convolution fusion | flops 504135680 | bytes 1462352 | tf_op jit(solution)/shard_map/hun,uhp->hpn/dot_general | solution.py:34
  15.4 1.3 copy.39
  16.7 7.3 %all-to-all-start = ((f32[20,8,1024]{2,0,1:T(8,128)}), f32[20,8,1024]{2,0,1:T(8,128)S(1)}, u32[]{:S(2)}, u32[]{:S(2)}) async-start(f32[20,8,1024]{2,0,1:T(8,128)} %copy.39), calls=%async_computation | async-start | bytes 1572864 | tf_op jit(solution)/shard_map/all_to_all | solution.py:116
  25.6 26.1 %all-reduce = f32[160]{0:T(256)S(1)} all-reduce(f32[160]{0:T(256)S(1)} %dynamic-update-slice), channel_id=2, replica_groups=mesh['seq'=8,'head'=4] {'seq'}, use_global_device_ids=true, to_apply=%add | all-reduce | flops 160 | bytes 1280
  53.9 0.7 slice_reduce_fusion.1
  54.7 1.4 %fusion.37 = pred[256,256]{1,0:T(8,128)(4,1)} fusion(pred[256]{0:T(512)(128)(4,1)} %copy-done.10), kind=kLoop, calls=%fused_computation.42 | loop fusion | flops 196608 | bytes 65792 | tf_op jit(solution)/shard_map/and | solution.py:16
  56.1 1.8 %fusion.43 = f32[256,256]{1,0:T(8,128)} fusion(bf16[256,128]{1,0:T(8,128)(2,1)} %param.13, bf16[256,128]{1,0:T(8,128)(2,1)} %param.14), kind=kOutput, calls=%fused_computation.64 | convolution fusion | flops 16777216 | bytes 393216 | tf_op jit(solution)/shard_map/dot_general | solution.py:19
  57.9 1.0 broadcast_in_dim.97
  58.9 11.4 %while.17 = (s32[]{:T(128)}, f32[20,1024]{1,0:T(8,128)S(1)}, f32[8,20,1024]{2,1,0:T(8,128)}, f32[8,20,1024]{2,1,0:T(8,128)S(1)}, f32[8,20]{1,0:T(8,128)}, /*index=5*/s32[]{:T(128)}, s32[]{:T(128)}, s32[]{:T(128)}) while((s32[]{:T(128)}, f32[20,1024]{1,0:T(8,128)S(1)}, f32[8,20,1024]{2,1,0:T(8,128)}, f32[8,20,1024]{2,1,0:T(8,128)S(1)}, ...), condition=%wide.region_3.4_spmd.clone, body=%wide.region_2.3_spmd.clone.sunk | while | flops 81924 | bytes 426352 | solution.py:118
  70.3 4.5 %all-to-all-start.1 = ((f32[20,8,1024]{2,0,1:T(8,128)}), f32[20,8,1024]{2,0,1:T(8,128)S(1)}, u32[]{:S(2)}, u32[]{:S(2)}) async-start(f32[20,8,1024]{2,0,1:T(8,128)} %bitcast.8), calls=%async_computation.1 | async-start | bytes 1572864 | tf_op jit(solution)/shard_map/all_to_all | solution.py:124
  74.8 2.8 %multiply_reduce_fusion.1 = f32[20,256]{1,0:T(8,128)} fusion(bf16[256,20,64]{0,2,1:T(8,128)(2,1)S(1)} %bitcast.81, f32[256,128]{0,1:T(8,128)} %copy-done.7, f32[1,20,64,128]{3,2,1,0:T(8,128)S(1)} %copy-done.2), kind=kOutput, calls=%fused_computation.17 | convolution fusion | flops 504622080 | bytes 1462272 | tf_op jit(solution)/shard_map/uhp,hpn->hun/dot_general | solution.py:35
  77.7 3.7 %fusion.21 = f32[256,20,64]{0,2,1:T(8,128)} fusion(bf16[256,20,64]{0,2,1:T(8,128)(2,1)S(1)} %bitcast.82, f32[256,256]{1,0:T(8,128)} %fusion.43, f32[20,256]{1,0:T(8,128)S(1)} %get-tuple-element.153, pred[256,256]{1,0:T(8,128)(4,1)} %fusion.37), kind=kOutput, calls=%fused_computation.29 | convolution fusion | flops 174325760 | bytes 2314240 | tf_op jit(solution)/shard_map/hsu,uhp->shp/dot_general | solution.py:24
  81.4 5.3 %multiply_reduce_fusion = (f32[20]{0:T(128)}, f32[20,256,256]{2,1,0:T(8,128)}) fusion(f32[20,256]{1,0:T(8,128)S(1)} %bitcast.86, f32[20,256]{1,0:T(8,128)S(1)} %copy-done.6, f32[256,256]{1,0:T(8,128)S(1)} %copy-done.5, f32[20,256]{1,0:T(8,128)S(1)} %get-tuple-element.153, pred[256,256]{1,0:T(8,128)(4,1)S(1)} %copy-done.8, ...), kind=kOutput, calls=%fused_computation.4 | convolution fusion | flops 179568624 | bytes 6942800 | tf_op jit(solution)/shard_map/shp,uhp->hsu/dot_general | solution.py:20
  86.8 5.5 %all-to-all-done.1 = f32[20,8,1024]{2,0,1:T(8,128)S(1)} async-done(((f32[20,8,1024]{2,0,1:T(8,128)}), f32[20,8,1024]{2,0,1:T(8,128)S(1)}, u32[]{:S(2)}, u32[]{:S(2)}) %all-to-all-start.1) | async-done | bytes 655392 | tf_op jit(solution)/shard_map/all_to_all | solution.py:124
  92.3 1.1 multiply_reduce_fusion.2
  93.4 2.8 %fusion.9 = (f32[20,256]{1,0:T(8,128)S(1)}, f32[20,128,256]{1,2,0:T(8,128)S(1)}) fusion(f32[256,128]{1,0:T(8,128)} %convert_element_type.21, f32[20,64,128]{2,1,0:T(8,128)S(1)} %reshape.294, bf16[256,20,64]{0,2,1:T(8,128)(2,1)S(1)} %bitcast.77), kind=kOutput, calls=%fused_computation.16 | convolution fusion | flops 504622080 | bytes 4083712 | tf_op jit(solution)/shard_map/shp,hpn->hsn/dot_general | solution.py:61
  96.5 5.2 %fusion.8 = f32[256,128]{1,0:T(8,128)} fusion(f32[20,128,256]{1,2,0:T(8,128)S(1)} %get-tuple-element.155, f32[20,256]{1,0:T(8,128)S(1)} %get-tuple-element.150, f32[20,256]{1,0:T(8,128)S(1)} %copy-done.6, f32[20,256,256]{2,1,0:T(8,128)} %get-tuple-element.157, f32[20,256]{1,0:T(8,128)S(1)} %get-tuple-element.153, pred[256,256]{1,0:T(8,128)(4,1)} %fusion.37, ...), kind=kOutput, calls=%fused_computation.15 | convolution fusion | flops 344686592 | bytes 8187904 | tf_op jit(solution)/shard_map/hsu,un->hsn/dot_general | solution.py:25
  102.4 19.4 %psum.15 = f32[20]{0:T(128)S(1)} all-reduce(f32[20]{0:T(128)S(1)} %multiply_add_fusion), channel_id=1, replica_groups=mesh['seq'=8,'head'=4] {'seq'}, use_global_device_ids=true, to_apply=%region_12.13 | all-reduce | flops 20 | bytes 160 | tf_op jit(solution)/shard_map/psum | solution.py:143
  121.8 1.1 copy.44
  123.4 9.1 %all-reduce.3.cloned.1.call-done = f32[256,128]{1,0:T(8,128)} async-done(((f32[256,128]{1,0:T(8,128)}), f32[256,128]{1,0:T(8,128)}) %all-reduce.3.cloned.1.call-update) | async-done | bytes 131088 | tf_op jit(solution)/shard_map/psum | solution.py:142
  132.6 1.6 %copy.62 = f32[256,128]{1,0:T(8,128)} copy(f32[256,128]{1,0:T(8,128)} %all-reduce.3.cloned.1.call-done) | data formatting | bytes 262144
  (98 shorter events, 18.6 us)
Async XLA Ops:
  7.2 16.8 %copy-start.20 = (u32[32]{0:T(128)S(1)}, u32[32]{0:T(128)}, u32[]{:S(2)}) copy-start(u32[32]{0:T(128)} %constant.57) | copy-start | bytes 388
  7.2 45.2 %copy-start.3 = (bf16[256,128]{1,0:T(8,128)(2,1)S(1)}, bf16[256,128]{1,0:T(8,128)(2,1)}, u32[]{:S(2)}) copy-start(bf16[256,128]{1,0:T(8,128)(2,1)} %param.13) | copy-start | bytes 196612
  7.2 45.8 %copy-start.1 = (bf16[256,1280]{1,0:T(8,128)(2,1)S(1)}, bf16[256,1280]{1,0:T(8,128)(2,1)}, u32[]{:S(2)}) copy-start(bf16[256,1280]{1,0:T(8,128)(2,1)} %param.10) | copy-start | bytes 1966084
  7.2 46.0 %copy-start.2 = (f32[1,20,64,128]{3,2,1,0:T(8,128)S(1)}, f32[1,20,64,128]{3,2,1,0:T(8,128)}, u32[]{:S(2)}) copy-start(f32[1,20,64,128]{3,2,1,0:T(8,128)} %param.16) | copy-start | bytes 1966084
  8.6 43.7 %copy-start.14 = (f32[20]{0:T(128)}, f32[20]{0:T(128)S(1)}, u32[]{:S(2)}) copy-start(f32[20]{0:T(128)S(1)} %neg.7) | copy-start | bytes 244
  10.9 41.4 %copy-start.10 = (pred[256]{0:T(512)(128)(4,1)}, pred[256]{0:T(512)(128)(4,1)S(1)}, u32[]{:S(2)}) copy-start(pred[256]{0:T(512)(128)(4,1)S(1)} %get-tuple-element.158) | copy-start | bytes 772
  11.2 41.1 %copy-start.11 = (f32[20]{0:T(128)}, f32[20]{0:T(128)S(1)}, u32[]{:S(2)}) copy-start(f32[20]{0:T(128)S(1)} %get-tuple-element.137) | copy-start | bytes 244
  12.2 1.4 copy-start.7
  16.7 41.2 %all-to-all-start = ((f32[20,8,1024]{2,0,1:T(8,128)}), f32[20,8,1024]{2,0,1:T(8,128)S(1)}, u32[]{:S(2)}, u32[]{:S(2)}) async-start(f32[20,8,1024]{2,0,1:T(8,128)} %copy.39), calls=%async_computation | async-start | bytes 1572864 | tf_op jit(solution)/shard_map/all_to_all | solution.py:116
  70.3 22.0 %all-to-all-start.1 = ((f32[20,8,1024]{2,0,1:T(8,128)}), f32[20,8,1024]{2,0,1:T(8,128)S(1)}, u32[]{:S(2)}, u32[]{:S(2)}) async-start(f32[20,8,1024]{2,0,1:T(8,128)} %bitcast.8), calls=%async_computation.1 | async-start | bytes 1572864 | tf_op jit(solution)/shard_map/all_to_all | solution.py:124
  74.8 57.8 %all-reduce.3.cloned.1.call-start = ((), (), s32[]{:S(2)}) async-start(), calls=%async_computation.2 | async-start | bytes 262144 | tf_op jit(solution)/shard_map/psum | solution.py:142
  77.7 3.7 %copy-start.5 = (f32[256,256]{1,0:T(8,128)S(1)}, f32[256,256]{1,0:T(8,128)}, u32[]{:S(2)}) copy-start(f32[256,256]{1,0:T(8,128)} %fusion.43) | copy-start | bytes 786436
  77.7 3.7 %copy-start.6 = (f32[20,256]{1,0:T(8,128)S(1)}, f32[20,256]{1,0:T(8,128)}, u32[]{:S(2)}) copy-start(f32[20,256]{1,0:T(8,128)} %param.11) | copy-start | bytes 61444
  77.7 3.7 %copy-start.8 = (pred[256,256]{1,0:T(8,128)(4,1)S(1)}, pred[256,256]{1,0:T(8,128)(4,1)}, u32[]{:S(2)}) copy-start(pred[256,256]{1,0:T(8,128)(4,1)} %fusion.37) | copy-start | bytes 196612
  86.8 9.4 %copy-start.9 = (f32[20,256]{1,0:T(8,128)S(1)}, f32[20,256]{1,0:T(8,128)}, u32[]{:S(2)}) copy-start(f32[20,256]{1,0:T(8,128)} %multiply_reduce_fusion.1) | copy-start | bytes 61444
  86.8 9.4 %copy-start.12 = (f32[20]{0:T(128)S(1)}, f32[20]{0:T(128)}, u32[]{:S(2)}) copy-start(f32[20]{0:T(128)} %copy-done.11) | copy-start | bytes 244
  86.8 9.5 %copy-start.13 = (f32[20]{0:T(128)S(1)}, f32[20]{0:T(128)}, u32[]{:S(2)}) copy-start(f32[20]{0:T(128)} %slice_reduce_fusion.1) | copy-start | bytes 244
  86.8 9.5 %copy-start.15 = (f32[20]{0:T(128)S(1)}, f32[20]{0:T(128)}, u32[]{:S(2)}) copy-start(f32[20]{0:T(128)} %copy-done.14) | copy-start | bytes 244
  86.8 9.5 %copy-start.16 = (pred[256]{0:T(512)(128)(4,1)S(1)}, pred[256]{0:T(512)(128)(4,1)}, u32[]{:S(2)}) copy-start(pred[256]{0:T(512)(128)(4,1)} %get-tuple-element.159) | copy-start | bytes 772
  86.8 9.5 %copy-start.18 = (pred[256]{0:T(512)(128)(4,1)S(1)}, pred[256]{0:T(512)(128)(4,1)}, u32[]{:S(2)}) copy-start(pred[256]{0:T(512)(128)(4,1)} %compare_bitcast_fusion) | copy-start | bytes 772
  96.5 5.2 %copy-start.17 = (f32[20]{0:T(128)S(1)}, f32[20]{0:T(128)}, u32[]{:S(2)}) copy-start(f32[20]{0:T(128)} %get-tuple-element.148) | copy-start | bytes 244
  96.5 5.2 %copy-start.19 = (f32[20]{0:T(128)S(1)}, f32[20]{0:T(128)}, u32[]{:S(2)}) copy-start(f32[20]{0:T(128)} %get-tuple-element.156) | copy-start | bytes 244
  96.5 5.2 %copy-start = (f32[256,20,64]{0,2,1:T(8,128)S(1)}, f32[256,20,64]{0,2,1:T(8,128)}, u32[]{:S(2)}) copy-start(f32[256,20,64]{0,2,1:T(8,128)} %fusion.21) | copy-start | bytes 3932164
  96.5 5.2 %copy-start.4 = (bf16[256,128]{1,0:T(8,128)(2,1)S(1)}, bf16[256,128]{1,0:T(8,128)(2,1)}, u32[]{:S(2)}) copy-start(bf16[256,128]{1,0:T(8,128)(2,1)} %param.13) | copy-start | bytes 196612
Sparse Core Ops, SparseCore 0:
  101.8 30.7 all-reduce.2
where the time goes:
time: 142 us; the launch traced here: 141 us
  blocking collectives  45.5 us (32%)
  matrix products  24 us (17%)
  local copies, waits for them, and re-layouts  16.6 us (12%)
  between operations  15.8 us (11%)
  waiting for transfers between devices  14.6 us (10%)
  other arithmetic  12.4 us (9%)
  starting transfers between devices  11.9 us (8%)
    unnamed x1, blocking collectives  26.1 us
    psum x1, blocking collectives, body(): grad_rate = -lax.psum(rate_total, 'seq')  19.4 us
    psum x1, waiting for transfers between devices, body(): grad_input_map = lax.psum(grad_b_list[0], 'head')  9.15 us
    all_to_all x1, starting transfers between devices, body(): lax.all_to_all(sliced, 'seq', split_axis=1, concat_axis=1, tiled=True)  7.31 us
    mul x8, local copies, waits for them, and re-layouts, backward_step(): return (grad_piece + gain_piece[:, None] * running, running)  5.48 us
    all_to_all x1, waiting for transfers between devices, body(): lax.all_to_all(jnp.transpose(exclusive, (1, 0, 2)), 'seq', split_axis=1,...  5.48 us
    dot_general x1, matrix products, prepare(): jnp.einsum('shp,uhp->hsu', x_block, grad_block, preferred_element_type=jn...  5.34 us
    unnamed x51, local copies, waits for them, and re-layouts  5.26 us
  transfers between devices with their start and end apart: 3, of which 2 were waited for; matrix products, arithmetic and copies ran while one was open for 15% of the time, Pallas kernels for 0%

commit v1 on v0

v1 whole, which is shorter than its diff:
```python
import functools

import jax
import jax.numpy as jnp
from jax import lax
from jax.experimental import pallas as pl
from jax.experimental.pallas import tpu as pltpu
from jax.sharding import PartitionSpec as P

MESH = pl.DeviceIdType.MESH
F32 = jnp.float32
BF16 = jnp.bfloat16
LANES = 128
LAG = 2


def split(value):
    high = value.astype(BF16)
    return high, (value - high.astype(F32)).astype(BF16)


def dot(a, b):
    return jnp.dot(a, b, preferred_element_type=F32)


def dot_nt(a, b):
    return lax.dot_general(a, b, (((1,), (1,)), ((), ())), preferred_element_type=F32)


def kernel(
    n, nh, width,
    x_ref, g_ref, dt_ref, dec_ref, b_ref, c_ref, s_ref, reset_ref,
    gx_ref, gb_ref, rate_ref,
    rows, ct, inter, acc, st, dxi, rate, bg, rxa, rxe, ebuf, ret, car,
    gbs, rxg, gsum, gfin, rtot, rxr,
    a_send, a_recv, e_send, e_recv, r_send, r_recv,
    g_send, g_recv, f_send, f_recv, t_send, t_recv,
):
    block_len = dt_ref.shape[1]
    head_count = dt_ref.shape[0]
    states = c_ref.shape[1]
    per = LANES // width
    chunks = head_count // per
    half = chunks // 2
    half_len = block_len // 2
    groups = n // 2
    me = lax.axis_index("seq")
    me_h = lax.axis_index("head")
    side = lax.rem(me, 2)
    group = lax.div(me, 2)
    partner = me + 1 - 2 * side
    below = jnp.maximum(me - 2, 0)
    last_group = group == groups - 1
    first_side = side == 0

    barrier = pltpu.get_barrier_semaphore()
    for d in range(1, n):
        pl.semaphore_signal(barrier, inc=1, device_id={"seq": lax.rem(me + d, n)}, device_id_type=MESH)
    for d in range(1, nh):
        pl.semaphore_signal(barrier, inc=1, device_id={"head": lax.rem(me_h + d, nh)}, device_id_type=MESH)

    reset_at = reset_ref[0]
    no_reset = reset_at >= block_len

    at_row = lax.broadcasted_iota(jnp.int32, (block_len, block_len), 0)
    at_col = lax.broadcasted_iota(jnp.int32, (block_len, block_len), 1)
    elapsed = jnp.dot(
        dt_ref[...], (at_row <= at_col).astype(F32),
        precision=lax.Precision.HIGHEST, preferred_element_type=F32,
    )
    for h in range(head_count):
        q, k = divmod(h, per)
        rows[q, k : k + 1, :] = elapsed[h : h + 1]
        rows[q, per + k : per + k + 1, :] = dt_ref[h : h + 1, :]
    ct[...] = c_ref[...].T
    joined = ((at_row >= reset_at) == (at_col >= reset_at)) & (at_col >= at_row)
    inter[...] = jnp.where(joined, dot_nt(b_ref[...], c_ref[...]), 0.0)
    acc[...] = jnp.zeros_like(acc)
    gbs[...] = jnp.zeros_like(gbs)

    @pl.when(last_group)
    def _():
        rxe[...] = jnp.zeros_like(rxe)

    lane_of = lax.broadcasted_iota(jnp.int32, (1, LANES), 1)

    def spread(items):
        out = items[0]
        for k in range(1, per):
            out = jnp.where(lane_of >= k * width, items[k], out)
        return out

    def columns(j):
        return rows[j].T

    def at(j):
        return pl.ds(pl.multiple_of(j * LANES, LANES), LANES)

    def lanes(cols, kind):
        return spread([cols[:, kind * per + k : kind * per + k + 1] for k in range(per)])

    def copy_a(jj):
        return pltpu.make_async_remote_copy(
            src_ref=bg.at[(1 - side) * half + jj], dst_ref=rxa.at[jj],
            send_sem=a_send.at[jj], recv_sem=a_recv.at[jj],
            device_id={"seq": partner}, device_id_type=MESH,
        )

    def copy_e(jj):
        return pltpu.make_async_remote_copy(
            src_ref=ebuf.at[jj], dst_ref=rxe.at[jj],
            send_sem=e_send.at[jj], recv_sem=e_recv.at[jj],
            device_id={"seq": below}, device_id_type=MESH,
        )

    def copy_r(jj):
        return pltpu.make_async_remote_copy(
            src_ref=ret.at[jj], dst_ref=car.at[side * half + jj],
            send_sem=r_send.at[jj], recv_sem=r_recv.at[jj],
            device_id={"seq": partner}, device_id_type=MESH,
        )

    def boundary(j):
        now = rows[j]
        row_of = lax.broadcasted_iota(jnp.int32, (per, block_len), 0)
        token = lax.broadcasted_iota(jnp.int32, (per, block_len), 1)
        later = token >= reset_at
        decay = jnp.full((per, block_len), dec_ref[j * per], F32)
        for k in range(1, per):
            decay = jnp.where(row_of == k, dec_ref[j * per + k], decay)
        log_decay = -decay * now[0:per]
        final = log_decay[:, block_len - 1 : block_len]
        rows[j, 2 * per : 3 * per, :] = jnp.where(later, 0.0, jnp.exp(log_decay))
        rows[j, 3 * per : 4 * per, :] = jnp.where(later | no_reset, jnp.exp(final - log_decay), 0.0)
        gain = jnp.where(no_reset, jnp.exp(final), 0.0)
        cols = columns(j)
        weighted = g_ref[:, at(j)].astype(F32) * lanes(cols, 2)
        high, low = split(weighted)
        bg[j, 0:states, :] = dot(ct[...], high) + dot(ct[...], low)
        gain_row = spread([gain[k : k + 1, :] for k in range(per)])
        bg[j, states : states + 8, :] = jnp.broadcast_to(gain_row, (8, LANES))

    boundary((1 - side) * half)
    pl.semaphore_wait(barrier, n + nh - 2)

    def give(jj, _):
        boundary((1 - side) * half + jj)
        copy_a(jj - 1).start()
        return 0

    lax.fori_loop(1, half, give, 0)
    boundary(side * half)
    copy_a(half - 1).start()

    def keep(jj, _):
        boundary(side * half + jj)
        return 0

    lax.fori_loop(1, half, keep, 0)

    def relay(jj):
        j = side * half + jj
        copy_a(jj).wait_recv()

        @pl.when(jnp.logical_not(last_group))
        def _():
            copy_e(jj).wait_recv()

        own = bg[j]
        other = rxa[jj]
        early = jnp.where(first_side, own, other)
        late = jnp.where(first_side, other, own)
        ending = rxe[jj]
        first = late[0:states] + late[states : states + 1] * ending

        @pl.when(group > 0)
        def _():
            ebuf[jj] = early[0:states] + early[states : states + 1] * first

        car[j] = jnp.where(first_side, first, ending)
        ret[jj] = jnp.where(first_side, ending, first)

        @pl.when(group > 0)
        def _():
            copy_e(jj).start()

        copy_r(jj).start()

    def pairs(j):
        now = rows[j]
        cols = columns(j)
        x_two = x_ref[:, at(j)]
        g_two = g_ref[:, at(j)]
        low_g = g_two[half_len:]
        inner = []
        terms = []
        for k in range(per):
            mine = (lane_of >= k * width) & (lane_of < (k + 1) * width)
            x_one = jnp.where(mine, x_two, jnp.zeros_like(x_two))
            rate_of = -dec_ref[j * per + k]
            parts = []
            total = jnp.zeros((1, LANES), F32)
            for top, left in ((0, 0), (half_len, half_len)):
                s_of = slice(top, top + half_len)
                u_of = slice(left, block_len)
                grad = g_two if left == 0 else low_g
                products = dot_nt(x_one[s_of], grad)
                gaps = now[k : k + 1, u_of] - cols[s_of, k : k + 1]
                gaps = jnp.maximum(gaps, 0.0)
                weight = jnp.exp(gaps * rate_of)
                mixing = weight * inter[s_of, u_of]
                scaled = weight * products * cols[s_of, per + k : per + k + 1]
                acc[s_of, u_of] += scaled
                parts.append(dot(mixing.astype(BF16), grad))
                inside = jnp.sum(mixing * gaps * products * cols[s_of, per + k : per + k + 1], axis=0, keepdims=True)
                for piece in range(0, inside.shape[1], LANES):
                    total = total + inside[:, piece : piece + LANES]
            inner.append(jnp.concatenate(parts, axis=0))
            shifted = total
            for k2 in range(1, per):
                shifted = shifted + pltpu.roll(total, k2 * width, 1)
            terms.append(shifted)
        dxi[j] = spread(inner)
        inside_row = spread(terms)
        state = s_ref[pl.ds(j * per, per)].reshape(LANES, states).T
        st[j] = state
        high, low = split(state)
        read = dot(c_ref[...], high) + dot(c_ref[...], low)
        entry = g_two.astype(F32) * read * (lanes(cols, 2) * lanes(cols, 0))
        entry_row = jnp.sum(entry, axis=0, keepdims=True)
        rate[j] = jnp.broadcast_to(inside_row + entry_row, (8, LANES))

    lag = (groups - 1 - group) * LAG

    def slot(t, _):
        jj = t - lag

        @pl.when((jj >= 0) & (jj < half))
        def _():
            relay(jj)

        @pl.when(t < chunks)
        def _():
            pairs(t)

        return 0

    lax.fori_loop(0, max(chunks, half + (groups - 1) * LAG), slot, 0)

    def finish(j):
        cols = columns(j)
        carried = car[j]
        high, low = split(carried)
        through = jnp.sum(carried * st[j], axis=0, keepdims=True)
        step = lanes(cols, 1)
        end = lanes(cols, 3)
        spent = lanes(cols, 0)
        last = spent[block_len - 1 : block_len]
        reach = end * (dot(b_ref[...], high) + dot(b_ref[...], low))
        gx_ref[:, at(j)] = (step * (dxi[j] + reach)).astype(BF16)
        x_step = x_ref[:, at(j)].astype(F32) * step
        leaving = jnp.sum(x_step * reach * (last - spent), axis=0, keepdims=True)
        x_high, x_low = split(x_step * end)
        gbs[...] += dot_nt(x_high, high) + dot_nt(x_high, low) + dot_nt(x_low, high)
        gain_row = bg[j, states : states + 1, :]
        rate[j] += jnp.broadcast_to(leaving + gain_row * last * through, (8, LANES))

    def closing(jj, _):
        finish(side * half + jj)
        pltpu.make_async_remote_copy(
            src_ref=ret.at[jj], dst_ref=car.at[(1 - side) * half + jj],
            send_sem=r_send.at[jj], recv_sem=r_recv.at[jj],
            device_id={"seq": partner}, device_id_type=MESH,
        ).wait_recv()
        finish((1 - side) * half + jj)
        return 0

    summed = jnp.where(joined, acc[...], 0.0)
    sum_high, sum_low = split(summed)
    gbs[...] += dot(sum_high, c_ref[...]) + dot(sum_low, c_ref[...])
    lax.fori_loop(0, half, closing, 0)

    share = block_len // nh

    def copy_g(d):
        peer = lax.rem(me_h + d, nh)
        return pltpu.make_async_remote_copy(
            src_ref=gbs.at[pl.ds(pl.multiple_of(peer * share, share), share)], dst_ref=rxg.at[d],
            send_sem=g_send.at[d], recv_sem=g_recv.at[d],
            device_id={"head": peer}, device_id_type=MESH,
        )

    def copy_f(d):
        peer = lax.rem(me_h + d, nh)
        return pltpu.make_async_remote_copy(
            src_ref=gsum, dst_ref=gfin.at[d],
            send_sem=f_send.at[d], recv_sem=f_recv.at[d],
            device_id={"head": peer}, device_id_type=MESH,
        )

    def copy_t(d):
        return pltpu.make_async_remote_copy(
            src_ref=rtot, dst_ref=rxr.at[d],
            send_sem=t_send.at[d], recv_sem=t_recv.at[d],
            device_id={"seq": lax.rem(me + d, n)}, device_id_type=MESH,
        )

    for d in range(1, nh):
        copy_g(d).start()

    parity = lax.broadcasted_iota(jnp.int32, (LANES, LANES), 0) // width
    target = lax.broadcasted_iota(jnp.int32, (LANES, LANES), 1)
    chosen = (lax.rem(target, per) == parity).astype(F32)
    folded = jnp.concatenate([rate[j, 0:1, :] for j in range(chunks)], axis=0)
    sums = jnp.dot(folded, chosen, precision=lax.Precision.HIGHEST, preferred_element_type=F32)
    home = lax.broadcasted_iota(jnp.int32, (chunks, LANES), 1) // per
    which = lax.broadcasted_iota(jnp.int32, (chunks, LANES), 0)
    mine_rate = jnp.sum(jnp.where(home == which, sums, 0.0), axis=0, keepdims=True)
    rtot[...] = jnp.broadcast_to(mine_rate, (8, LANES))

    own_share = gbs[pl.ds(pl.multiple_of(me_h * share, share), share), :]
    for d in range(1, n):
        copy_t(d).start()
    for d in range(1, nh):
        copy_g(d).wait_recv()
        own_share = own_share + rxg[d]
    gsum[...] = own_share
    gb_ref[pl.ds(pl.multiple_of(me_h * share, share), share), :] = own_share
    for d in range(1, nh):
        copy_f(d).start()
    all_rate = rtot[...]
    for d in range(1, n):
        copy_t(d).wait_recv()
        all_rate = all_rate + rxr[d]
    rate_ref[...] = -all_rate
    for d in range(1, nh):
        copy_f(d).wait_recv()
        source = lax.rem(me_h + nh - d, nh)
        gb_ref[pl.ds(pl.multiple_of(source * share, share), share), :] = gfin[d]

    for jj in range(half):
        copy_a(jj).wait_send()
        copy_r(jj).wait_send()

    @pl.when(group > 0)
    def _():
        for jj in range(half):
            copy_e(jj).wait_send()

    for d in range(1, nh):
        copy_g(d).wait_send()
        copy_f(d).wait_send()
    for d in range(1, n):
        copy_t(d).wait_send()


def body(n, nh, inputs, time_step, decay_rate, input_map, output_map, output_grad, span_states, resets):
    head_count, block_len = time_step.shape
    width, states = span_states.shape[2:]
    chunks = inputs.shape[1] // LANES
    half = chunks // 2
    share = block_len // nh
    vmem = pl.BlockSpec(memory_space=pltpu.VMEM)
    smem = pl.BlockSpec(memory_space=pltpu.SMEM)
    sem = pltpu.SemaphoreType.DMA
    grad_inputs, grad_map, rates = pl.pallas_call(
        functools.partial(kernel, n, nh, width),
        out_shape=(
            jax.ShapeDtypeStruct(inputs.shape, BF16),
            jax.ShapeDtypeStruct((block_len, states), F32),
            jax.ShapeDtypeStruct((8, LANES), F32),
        ),
        in_specs=[vmem, vmem, vmem, smem, vmem, vmem, vmem, smem],
        out_specs=(vmem, vmem, vmem),
        scratch_shapes=[
            pltpu.VMEM((chunks, 8, block_len), F32),
            pltpu.VMEM((states, block_len), BF16),
            pltpu.VMEM((block_len, block_len), F32),
            pltpu.VMEM((block_len, block_len), F32),
            pltpu.VMEM((chunks, states, LANES), F32),
            pltpu.VMEM((chunks, block_len, LANES), F32),
            pltpu.VMEM((chunks, 8, LANES), F32),
            pltpu.VMEM((chunks, states + 8, LANES), F32),
            pltpu.VMEM((half, states + 8, LANES), F32),
            pltpu.VMEM((half, states, LANES), F32),
            pltpu.VMEM((half, states, LANES), F32),
            pltpu.VMEM((half, states, LANES), F32),
            pltpu.VMEM((chunks, states, LANES), F32),
            pltpu.VMEM((block_len, states), F32),
            pltpu.VMEM((nh, share, states), F32),
            pltpu.VMEM((share, states), F32),
            pltpu.VMEM((nh, share, states), F32),
            pltpu.VMEM((8, LANES), F32),
            pltpu.VMEM((n, 8, LANES), F32),
            sem((half,)), sem((half,)), sem((half,)), sem((half,)), sem((half,)), sem((half,)),
            sem((nh,)), sem((nh,)), sem((nh,)), sem((nh,)), sem((n,)), sem((n,)),
        ],
        compiler_params=pltpu.CompilerParams(
            collective_id=0, has_side_effects=True, vmem_limit_bytes=48 * 2**20
        ),
    )(inputs, output_grad, time_step, decay_rate, input_map, output_map, span_states[0], resets)
    return grad_inputs, grad_map, rates[0, :head_count]


def solution(mesh):
    in_specs = (
        P("seq", "head"),
        P("head", "seq"),
        P("head"),
        P("seq", None),
        P("seq", None),
        P("seq", "head"),
        P("seq", "head", None, None),
        P("seq"),
    )
    out_specs = (P("seq", "head"), P("seq", None), P("head"))
    run = functools.partial(body, mesh.shape["seq"], mesh.shape["head"])
    return jax.shard_map(run, mesh=mesh, in_specs=in_specs, out_specs=out_specs, check_vma=False)
```

time: 142 us -> 48.6 us (0.34)
  blocking collectives: 45.5 us -> 0 us
  Pallas kernels: 0 us -> 38.6 us
  matrix products: 24 us -> 0 us
  waiting for transfers between devices: 14.6 us -> 0 us
  between operations: 15.8 us -> 1.3 us
  other arithmetic: 12.4 us -> 0 us
  starting transfers between devices: 11.9 us -> 0 us
  local copies, waits for them, and re-layouts: 16.6 us -> 8.33 us
    pallas_call x0 -> x1, Pallas kernels: none -> 38.6 us  [body(): pl.pallas_call(functools.partial(kernel, n, nh, width), out_shape=(jax.Sh...]
    unnamed x1 -> x0, blocking collectives: 26.1 us -> none
    dot_general x8 -> x0, matrix products: 24 us -> none  [the longest x1 5.34 us: prepare(): jnp.einsum('shp,uhp->hsu', x_block, grad_block, preferred_element_type=jn...]
    psum x1 -> x0, blocking collectives: 19.4 us -> none  [body(): grad_rate = -lax.psum(rate_total, 'seq')]
    all_to_all x2 -> x0, starting transfers between devices: 11.8 us -> none  [the longest x1 7.31 us: body(): lax.all_to_all(sliced, 'seq', split_axis=1, concat_axis=1, tiled=True)]
    psum x1 -> x0, waiting for transfers between devices: 9.15 us -> none  [body(): grad_input_map = lax.psum(grad_b_list[0], 'head')]
    all_to_all x2 -> x0, waiting for transfers between devices: 5.48 us -> none  [the longest x1 5.48 us: body(): lax.all_to_all(jnp.transpose(exclusive, (1, 0, 2)), 'seq', split_axis=1,...]
    mul x8 -> x0, local copies, waits for them, and re-layouts: 5.48 us -> none  [backward_step(): return (grad_piece + gain_piece[:, None] * running, running)]
  transfers between devices with their start and end apart: 3 -> 0, of which waited for: 2 -> 0; matrix products, arithmetic and copies ran while one was open for 15% -> 0% of each run, Pallas kernels for 0% -> 0%
where the time goes in v1:
time: 48.6 us; the launch traced here: 48.2 us
  Pallas kernels  38.6 us (79%)
  local copies, waits for them, and re-layouts  8.33 us (17%)
  between operations  1.3 us (3%)
    pallas_call x1, Pallas kernels, body(): pl.pallas_call(functools.partial(kernel, n, nh, width), out_shape=(jax.Sh...  38.6 us
    unnamed x16, local copies, waits for them, and re-layouts  7.81 us

profile of v1, /device:TPU:0, one launch (start us, length us, event | category | flops | bytes accessed | tf_op | source)
XLA Modules:
  0.0 48.2 jit_solution(8594822356742518936)
XLA Ops:
  1.3 0.0 copy-start.6
  1.3 0.6 %copy-done.6 = f32[20]{0:T(128)S(1)} copy-done((f32[20]{0:T(128)S(1)}, f32[20]{0:T(128)}, u32[]{:S(2)}) %copy-start.6) | copy-done | bytes 104
  1.9 0.0 copy-start
  1.9 1.1 %copy-done = bf16[256,1280]{1,0:T(8,128)(2,1)S(1)} copy-done((bf16[256,1280]{1,0:T(8,128)(2,1)S(1)}, bf16[256,1280]{1,0:T(8,128)(2,1)}, u32[]{:S(2)}) %copy-start) | copy-done | bytes 655384
  3.0 0.0 copy-start.1
  3.0 1.1 %copy-done.1 = bf16[256,1280]{1,0:T(8,128)(2,1)S(1)} copy-done((bf16[256,1280]{1,0:T(8,128)(2,1)S(1)}, bf16[256,1280]{1,0:T(8,128)(2,1)}, u32[]{:S(2)}) %copy-start.1) | copy-done | bytes 655384
  4.1 0.0 copy-start.2
  4.1 1.1 %copy-done.2 = f32[1,20,64,128]{3,2,1,0:T(8,128)S(1)} copy-done((f32[1,20,64,128]{3,2,1,0:T(8,128)S(1)}, f32[1,20,64,128]{3,2,1,0:T(8,128)}, u32[]{:S(2)}) %copy-start.2) | copy-done | bytes 655384
  5.2 0.0 copy-start.3
  5.2 0.8 %copy-done.3 = bf16[256,128]{1,0:T(8,128)(2,1)S(1)} copy-done((bf16[256,128]{1,0:T(8,128)(2,1)S(1)}, bf16[256,128]{1,0:T(8,128)(2,1)}, u32[]{:S(2)}) %copy-start.3) | copy-done | bytes 65560
  6.0 0.0 copy-start.4
  6.0 0.8 %copy-done.4 = bf16[256,128]{1,0:T(8,128)(2,1)S(1)} copy-done((bf16[256,128]{1,0:T(8,128)(2,1)S(1)}, bf16[256,128]{1,0:T(8,128)(2,1)}, u32[]{:S(2)}) %copy-start.4) | copy-done | bytes 65560
  6.9 0.0 copy-start.5
  6.9 0.7 %copy-done.5 = f32[20,256]{1,0:T(8,128)S(1)} copy-done((f32[20,256]{1,0:T(8,128)S(1)}, f32[20,256]{1,0:T(8,128)}, u32[]{:S(2)}) %copy-start.5) | copy-done | bytes 20504
  7.6 38.6 %shard_map.103 = (bf16[256,1280]{1,0:T(8,128)(2,1)S(1)}, f32[256,128]{1,0:T(8,128)S(1)}, f32[8,128]{1,0:T(8,128)S(1)}) custom-call(bf16[256,1280]{1,0:T(8,128)(2,1)S(1)} %copy-done, bf16[256,1280]{1,0:T(8,128)(2,1)S(1)} %copy-done.1, f32[20,256]{1,0:T(8,128)S(1)} %copy-done.5, f32[20]{0:T(128)S(1)} %copy-done.6, bf16[256,128]{1,0:T(8,128)(2,1)S(1)} %copy-done.3, ...), custom_call_target="tpu_custom_call" | custom-call | tf_op jit(solution)/shard_map/pallas_call | solution.py:366
  46.2 0.5 %slice_bitcast_fusion = f32[20]{0:T(128)} fusion(f32[8,128]{1,0:T(8,128)S(1)} %get-tuple-element.8), kind=kLoop, calls=%fused_computation | loop fusion | bytes 160 | tf_op jit(solution)/shard_map/squeeze | solution.py:402
  46.7 0.8 %copy.14 = bf16[256,1280]{1,0:T(8,128)(2,1)} copy(bf16[256,1280]{1,0:T(8,128)(2,1)S(1)} %get-tuple-element.12) | data formatting | bytes 1310720
  47.5 0.7 %copy.15 = f32[256,128]{1,0:T(8,128)} copy(f32[256,128]{1,0:T(8,128)S(1)} %get-tuple-element.13) | data formatting | bytes 262144
Async XLA Ops:
  1.3 0.7 %copy-start.6 = (f32[20]{0:T(128)S(1)}, f32[20]{0:T(128)}, u32[]{:S(2)}) copy-start(f32[20]{0:T(128)} %dec_ref.1) | copy-start | bytes 244
  1.9 1.1 %copy-start = (bf16[256,1280]{1,0:T(8,128)(2,1)S(1)}, bf16[256,1280]{1,0:T(8,128)(2,1)}, u32[]{:S(2)}) copy-start(bf16[256,1280]{1,0:T(8,128)(2,1)} %x_ref.1) | copy-start | bytes 1966084
  3.0 1.1 %copy-start.1 = (bf16[256,1280]{1,0:T(8,128)(2,1)S(1)}, bf16[256,1280]{1,0:T(8,128)(2,1)}, u32[]{:S(2)}) copy-start(bf16[256,1280]{1,0:T(8,128)(2,1)} %g_ref.1) | copy-start | bytes 1966084
  4.1 1.1 %copy-start.2 = (f32[1,20,64,128]{3,2,1,0:T(8,128)S(1)}, f32[1,20,64,128]{3,2,1,0:T(8,128)}, u32[]{:S(2)}) copy-start(f32[1,20,64,128]{3,2,1,0:T(8,128)} %param.14) | copy-start | bytes 1966084
  5.2 0.8 %copy-start.3 = (bf16[256,128]{1,0:T(8,128)(2,1)S(1)}, bf16[256,128]{1,0:T(8,128)(2,1)}, u32[]{:S(2)}) copy-start(bf16[256,128]{1,0:T(8,128)(2,1)} %b_ref.1) | copy-start | bytes 196612
  6.0 0.8 %copy-start.4 = (bf16[256,128]{1,0:T(8,128)(2,1)S(1)}, bf16[256,128]{1,0:T(8,128)(2,1)}, u32[]{:S(2)}) copy-start(bf16[256,128]{1,0:T(8,128)(2,1)} %c_ref.1) | copy-start | bytes 196612
  6.9 0.7 %copy-start.5 = (f32[20,256]{1,0:T(8,128)S(1)}, f32[20,256]{1,0:T(8,128)}, u32[]{:S(2)}) copy-start(f32[20,256]{1,0:T(8,128)} %dt_ref.1) | copy-start | bytes 61444

commit v2 on v1

--- a/solution.py
+++ b/solution.py
@@ -11,7 +11,9 @@
 F32 = jnp.float32
 BF16 = jnp.bfloat16
 LANES = 128
-LAG = 2
+LAG = 3
+GAIN_ROWS = 8
+PIECES = 2
 
 
 def split(value):
@@ -29,13 +31,21 @@
 
 def kernel(
     n, nh, width,
-    x_ref, g_ref, dt_ref, dec_ref, b_ref, c_ref, s_ref, reset_ref,
+    x_in, g_in, dt_in, dec_in, b_in, c_in, s_in, reset_in,
     gx_ref, gb_ref, rate_ref,
+    x_ref, g_ref, dt_ref, dec_ref, b_ref, c_ref, s_ref, reset_ref, in_sem,
     rows, ct, inter, acc, st, dxi, rate, bg, rxa, rxe, ebuf, ret, car,
     gbs, rxg, gsum, gfin, rtot, rxr,
     a_send, a_recv, e_send, e_recv, r_send, r_recv,
     g_send, g_recv, f_send, f_recv, t_send, t_recv,
 ):
+    loads = {}
+    names = ("dt", "dec", "reset", "c", "g", "b", "x", "s")
+    places = ((dt_in, dt_ref), (dec_in, dec_ref), (reset_in, reset_ref), (c_in, c_ref),
+              (g_in, g_ref), (b_in, b_ref), (x_in, x_ref), (s_in, s_ref))
+    for number, (source, target) in enumerate(places):
+        loads[names[number]] = pltpu.make_async_copy(source, target, in_sem.at[number])
+        loads[names[number]].start()
     block_len = dt_ref.shape[1]
     head_count = dt_ref.shape[0]
     states = c_ref.shape[1]
@@ -59,11 +69,14 @@
     for d in range(1, nh):
         pl.semaphore_signal(barrier, inc=1, device_id={"head": lax.rem(me_h + d, nh)}, device_id_type=MESH)
 
+    loads["dec"].wait()
+    loads["reset"].wait()
     reset_at = reset_ref[0]
     no_reset = reset_at >= block_len
 
     at_row = lax.broadcasted_iota(jnp.int32, (block_len, block_len), 0)
     at_col = lax.broadcasted_iota(jnp.int32, (block_len, block_len), 1)
+    loads["dt"].wait()
     elapsed = jnp.dot(
         dt_ref[...], (at_row <= at_col).astype(F32),
         precision=lax.Precision.HIGHEST, preferred_element_type=F32,
@@ -72,16 +85,8 @@
         q, k = divmod(h, per)
         rows[q, k : k + 1, :] = elapsed[h : h + 1]
         rows[q, per + k : per + k + 1, :] = dt_ref[h : h + 1, :]
+    loads["c"].wait()
     ct[...] = c_ref[...].T
-    joined = ((at_row >= reset_at) == (at_col >= reset_at)) & (at_col >= at_row)
-    inter[...] = jnp.where(joined, dot_nt(b_ref[...], c_ref[...]), 0.0)
-    acc[...] = jnp.zeros_like(acc)
-    gbs[...] = jnp.zeros_like(gbs)
-
-    @pl.when(last_group)
-    def _():
-        rxe[...] = jnp.zeros_like(rxe)
-
     lane_of = lax.broadcasted_iota(jnp.int32, (1, LANES), 1)
 
     def spread(items):
@@ -99,24 +104,33 @@
     def lanes(cols, kind):
         return spread([cols[:, kind * per + k : kind * per + k + 1] for k in range(per)])
 
-    def copy_a(jj):
-        return pltpu.make_async_remote_copy(
-            src_ref=bg.at[(1 - side) * half + jj], dst_ref=rxa.at[jj],
-            send_sem=a_send.at[jj], recv_sem=a_recv.at[jj],
+    part = states // PIECES
+
+    def span(p):
+        begin = GAIN_ROWS + p * part if p else 0
+        return pl.ds(begin, GAIN_ROWS + (p + 1) * part - begin)
+
+    def of(p):
+        return pl.ds(p * part, part)
+
+    def copy_a(jj, p):
+        return pltpu.make_async_remote_copy(
+            src_ref=bg.at[(1 - side) * half + jj, span(p)], dst_ref=rxa.at[jj, span(p)],
+            send_sem=a_send.at[jj, p], recv_sem=a_recv.at[jj, p],
             device_id={"seq": partner}, device_id_type=MESH,
         )
 
-    def copy_e(jj):
-        return pltpu.make_async_remote_copy(
-            src_ref=ebuf.at[jj], dst_ref=rxe.at[jj],
-            send_sem=e_send.at[jj], recv_sem=e_recv.at[jj],
+    def copy_e(jj, p):
+        return pltpu.make_async_remote_copy(
+            src_ref=ebuf.at[jj, of(p)], dst_ref=rxe.at[jj, of(p)],
+            send_sem=e_send.at[jj, p], recv_sem=e_recv.at[jj, p],
             device_id={"seq": below}, device_id_type=MESH,
         )
 
-    def copy_r(jj):
-        return pltpu.make_async_remote_copy(
-            src_ref=ret.at[jj], dst_ref=car.at[side * half + jj],
-            send_sem=r_send.at[jj], recv_sem=r_recv.at[jj],
+    def copy_r(jj, p, holder):
+        return pltpu.make_async_remote_copy(
+            src_ref=ret.at[jj, of(p)], dst_ref=car.at[holder * half + jj, of(p)],
+            send_sem=r_send.at[jj, p], recv_sem=r_recv.at[jj, p],
             device_id={"seq": partner}, device_id_type=MESH,
         )
 
@@ -136,21 +150,24 @@
         cols = columns(j)
         weighted = g_ref[:, at(j)].astype(F32) * lanes(cols, 2)
         high, low = split(weighted)
-        bg[j, 0:states, :] = dot(ct[...], high) + dot(ct[...], low)
+        bg[j, GAIN_ROWS : GAIN_ROWS + states, :] = dot(ct[...], high) + dot(ct[...], low)
         gain_row = spread([gain[k : k + 1, :] for k in range(per)])
-        bg[j, states : states + 8, :] = jnp.broadcast_to(gain_row, (8, LANES))
-
+        bg[j, 0:GAIN_ROWS, :] = jnp.broadcast_to(gain_row, (GAIN_ROWS, LANES))
+
+    loads["g"].wait()
     boundary((1 - side) * half)
     pl.semaphore_wait(barrier, n + nh - 2)
 
     def give(jj, _):
         boundary((1 - side) * half + jj)
-        copy_a(jj - 1).start()
+        for p in range(PIECES):
+            copy_a(jj - 1, p).start()
         return 0
 
     lax.fori_loop(1, half, give, 0)
     boundary(side * half)
-    copy_a(half - 1).start()
+    for p in range(PIECES):
+        copy_a(half - 1, p).start()
 
     def keep(jj, _):
         boundary(side * half + jj)
@@ -158,33 +175,53 @@
 
     lax.fori_loop(1, half, keep, 0)
 
+    loads["b"].wait()
+    joined = ((at_row >= reset_at) == (at_col >= reset_at)) & (at_col >= at_row)
+    inter[...] = jnp.where(joined, dot_nt(b_ref[...], c_ref[...]), 0.0)
+    acc[...] = jnp.zeros_like(acc)
+    gbs[...] = jnp.zeros_like(gbs)
+
+    @pl.when(last_group)
+    def _():
+        rxe[...] = jnp.zeros_like(rxe)
+
+    loads["x"].wait()
+    loads["s"].wait()
+
     def relay(jj):
         j = side * half + jj
-        copy_a(jj).wait_recv()
-
-        @pl.when(jnp.logical_not(last_group))
-        def _():
-            copy_e(jj).wait_recv()
-
-        own = bg[j]
-        other = rxa[jj]
-        early = jnp.where(first_side, own, other)
-        late = jnp.where(first_side, other, own)
-        ending = rxe[jj]
-        first = late[0:states] + late[states : states + 1] * ending
-
-        @pl.when(group > 0)
-        def _():
-            ebuf[jj] = early[0:states] + early[states : states + 1] * first
-
-        car[j] = jnp.where(first_side, first, ending)
-        ret[jj] = jnp.where(first_side, ending, first)
-
-        @pl.when(group > 0)
-        def _():
-            copy_e(jj).start()
-
-        copy_r(jj).start()
+        for p in range(PIECES):
+            copy_a(jj, p).wait_recv()
+
+            @pl.when(jnp.logical_not(last_group))
+            def _():
+                copy_e(jj, p).wait_recv()
+
+            if p == 0:
+                own_gain = bg[j, 0:1, :]
+                other_gain = rxa[jj, 0:1, :]
+                early_gain = jnp.where(first_side, own_gain, other_gain)
+                late_gain = jnp.where(first_side, other_gain, own_gain)
+            here = pl.ds(GAIN_ROWS + p * part, part)
+            own = bg[j, here, :]
+            other = rxa[jj, here, :]
+            early = jnp.where(first_side, own, other)
+            late = jnp.where(first_side, other, own)
+            ending = rxe[jj, of(p), :]
+            first = late + late_gain * ending
+
+            @pl.when(group > 0)
+            def _():
+                ebuf[jj, of(p), :] = early + early_gain * first
+
+            car[j, of(p), :] = jnp.where(first_side, first, ending)
+            ret[jj, of(p), :] = jnp.where(first_side, ending, first)
+
+            @pl.when(group > 0)
+            def _():
+                copy_e(jj, p).start()
+
+            copy_r(jj, p, side).start()
 
     def pairs(j):
         now = rows[j]
@@ -230,23 +267,6 @@
         entry_row = jnp.sum(entry, axis=0, keepdims=True)
         rate[j] = jnp.broadcast_to(inside_row + entry_row, (8, LANES))
 
-    lag = (groups - 1 - group) * LAG
-
-    def slot(t, _):
-        jj = t - lag
-
-        @pl.when((jj >= 0) & (jj < half))
-        def _():
-            relay(jj)
-
-        @pl.when(t < chunks)
-        def _():
-            pairs(t)
-
-        return 0
-
-    lax.fori_loop(0, max(chunks, half + (groups - 1) * LAG), slot, 0)
-
     def finish(j):
         cols = columns(j)
         carried = car[j]
@@ -262,23 +282,42 @@
         leaving = jnp.sum(x_step * reach * (last - spent), axis=0, keepdims=True)
         x_high, x_low = split(x_step * end)
         gbs[...] += dot_nt(x_high, high) + dot_nt(x_high, low) + dot_nt(x_low, high)
-        gain_row = bg[j, states : states + 1, :]
+        gain_row = bg[j, 0:1, :]
         rate[j] += jnp.broadcast_to(leaving + gain_row * last * through, (8, LANES))
 
-    def closing(jj, _):
-        finish(side * half + jj)
-        pltpu.make_async_remote_copy(
-            src_ref=ret.at[jj], dst_ref=car.at[(1 - side) * half + jj],
-            send_sem=r_send.at[jj], recv_sem=r_recv.at[jj],
-            device_id={"seq": partner}, device_id_type=MESH,
-        ).wait_recv()
-        finish((1 - side) * half + jj)
+    base = max(chunks - 1, (groups - 1) * LAG)
+    lag = base - group * LAG
+
+    def slot(t, _):
+        jj = t - lag
+
+        @pl.when((jj >= 0) & (jj < half))
+        def _():
+            relay(jj)
+
+        @pl.when(t < chunks)
+        def _():
+            pairs(t)
+
+        @pl.when((t >= base) & (t < base + half))
+        def _():
+            finish(side * half + t - base)
+
+        late = t - base - 2
+
+        @pl.when(late >= 0)
+        def _():
+            for p in range(PIECES):
+                copy_r(late, p, 1 - side).wait_recv()
+            finish((1 - side) * half + late)
+
         return 0
 
+    lax.fori_loop(0, base + half, slot, 0)
     summed = jnp.where(joined, acc[...], 0.0)
     sum_high, sum_low = split(summed)
     gbs[...] += dot(sum_high, c_ref[...]) + dot(sum_low, c_ref[...])
-    lax.fori_loop(0, half, closing, 0)
+    lax.fori_loop(base + half, base + half + 2, slot, 0)
 
     share = block_len // nh
 
@@ -339,13 +378,15 @@
         gb_ref[pl.ds(pl.multiple_of(source * share, share), share), :] = gfin[d]
 
     for jj in range(half):
-        copy_a(jj).wait_send()
-        copy_r(jj).wait_send()
+        for p in range(PIECES):
+            copy_a(jj, p).wait_send()
+            copy_r(jj, p, side).wait_send()
 
     @pl.when(group > 0)
     def _():
         for jj in range(half):
-            copy_e(jj).wait_send()
+            for p in range(PIECES):
+                copy_e(jj, p).wait_send()
 
     for d in range(1, nh):
         copy_g(d).wait_send()
@@ -361,7 +402,7 @@
     half = chunks // 2
     share = block_len // nh
     vmem = pl.BlockSpec(memory_space=pltpu.VMEM)
-    smem = pl.BlockSpec(memory_space=pltpu.SMEM)
+    hbm = pl.BlockSpec(memory_space=pltpu.HBM)
     sem = pltpu.SemaphoreType.DMA
     grad_inputs, grad_map, rates = pl.pallas_call(
         functools.partial(kernel, n, nh, width),
@@ -370,9 +411,18 @@
             jax.ShapeDtypeStruct((block_len, states), F32),
             jax.ShapeDtypeStruct((8, LANES), F32),
         ),
-        in_specs=[vmem, vmem, vmem, smem, vmem, vmem, vmem, smem],
+        in_specs=[hbm] * 8,
         out_specs=(vmem, vmem, vmem),
         scratch_shapes=[
+            pltpu.VMEM(inputs.shape, BF16),
+            pltpu.VMEM(inputs.shape, BF16),
+            pltpu.VMEM(time_step.shape, F32),
+            pltpu.SMEM(decay_rate.shape, F32),
+            pltpu.VMEM(input_map.shape, BF16),
+            pltpu.VMEM(output_map.shape, BF16),
+            pltpu.VMEM(span_states.shape[1:], F32),
+            pltpu.SMEM(resets.shape, jnp.int32),
+            sem((8,)),
             pltpu.VMEM((chunks, 8, block_len), F32),
             pltpu.VMEM((states, block_len), BF16),
             pltpu.VMEM((block_len, block_len), F32),
@@ -380,8 +430,8 @@
             pltpu.VMEM((chunks, states, LANES), F32),
             pltpu.VMEM((chunks, block_len, LANES), F32),
             pltpu.VMEM((chunks, 8, LANES), F32),
-            pltpu.VMEM((chunks, states + 8, LANES), F32),
-            pltpu.VMEM((half, states + 8, LANES), F32),
+            pltpu.VMEM((chunks, states + GAIN_ROWS, LANES), F32),
+            pltpu.VMEM((half, states + GAIN_ROWS, LANES), F32),
             pltpu.VMEM((half, states, LANES), F32),
             pltpu.VMEM((half, states, LANES), F32),
             pltpu.VMEM((half, states, LANES), F32),
@@ -392,13 +442,13 @@
             pltpu.VMEM((nh, share, states), F32),
             pltpu.VMEM((8, LANES), F32),
             pltpu.VMEM((n, 8, LANES), F32),
-            sem((half,)), sem((half,)), sem((half,)), sem((half,)), sem((half,)), sem((half,)),
+            *[sem((half, PIECES)) for _ in range(6)],
             sem((nh,)), sem((nh,)), sem((nh,)), sem((nh,)), sem((n,)), sem((n,)),
         ],
         compiler_params=pltpu.CompilerParams(
-            collective_id=0, has_side_effects=True, vmem_limit_bytes=48 * 2**20
+            collective_id=0, has_side_effects=True, vmem_limit_bytes=40 * 2**20
         ),
-    )(inputs, output_grad, time_step, decay_rate, input_map, output_map, span_states[0], resets)
+    )(inputs, output_grad, time_step, decay_rate, input_map, output_map, span_states.reshape(span_states.shape[1:]), resets)
     return grad_inputs, grad_map, rates[0, :head_count]
 
 

time: 48.6 us -> 47.1 us (0.969)
  Pallas kernels: 38.6 us -> 37 us
    pallas_call x1, Pallas kernels: 38.6 us -> 37 us  [body(): pl.pallas_call(functools.partial(kernel, n, nh, width), out_shape=(jax.Sh...]
where the time goes in v2:
time: 47.1 us; the launch traced here: 46.6 us
  Pallas kernels  37 us (79%)
  local copies, waits for them, and re-layouts  8.33 us (18%)
  between operations  1.3 us (3%)
    pallas_call x1, Pallas kernels, body(): pl.pallas_call(functools.partial(kernel, n, nh, width), out_shape=(jax.Sh...  37 us
    unnamed x16, local copies, waits for them, and re-layouts  7.81 us

profile of v2, /device:TPU:0, one launch (start us, length us, event | category | flops | bytes accessed | tf_op | source)
XLA Modules:
  0.0 46.6 jit_solution(15078186882216214387)
XLA Ops:
  1.3 0.0 copy-start.6
  1.3 0.6 %copy-done.6 = f32[20]{0:T(128)S(1)} copy-done((f32[20]{0:T(128)S(1)}, f32[20]{0:T(128)}, u32[]{:S(2)}) %copy-start.6) | copy-done | bytes 104
  1.9 0.0 copy-start
  1.9 1.1 %copy-done = bf16[256,1280]{1,0:T(8,128)(2,1)S(1)} copy-done((bf16[256,1280]{1,0:T(8,128)(2,1)S(1)}, bf16[256,1280]{1,0:T(8,128)(2,1)}, u32[]{:S(2)}) %copy-start) | copy-done | bytes 655384
  3.0 0.0 copy-start.1
  3.0 1.1 %copy-done.1 = bf16[256,1280]{1,0:T(8,128)(2,1)S(1)} copy-done((bf16[256,1280]{1,0:T(8,128)(2,1)S(1)}, bf16[256,1280]{1,0:T(8,128)(2,1)}, u32[]{:S(2)}) %copy-start.1) | copy-done | bytes 655384
  4.1 0.0 copy-start.2
  4.1 1.1 %copy-done.2 = f32[1,20,64,128]{3,2,1,0:T(8,128)S(1)} copy-done((f32[1,20,64,128]{3,2,1,0:T(8,128)S(1)}, f32[1,20,64,128]{3,2,1,0:T(8,128)}, u32[]{:S(2)}) %copy-start.2) | copy-done | bytes 655384
  5.2 0.0 copy-start.3
  5.2 0.8 %copy-done.3 = bf16[256,128]{1,0:T(8,128)(2,1)S(1)} copy-done((bf16[256,128]{1,0:T(8,128)(2,1)S(1)}, bf16[256,128]{1,0:T(8,128)(2,1)}, u32[]{:S(2)}) %copy-start.3) | copy-done | bytes 65560
  6.0 0.0 copy-start.4
  6.0 0.8 %copy-done.4 = bf16[256,128]{1,0:T(8,128)(2,1)S(1)} copy-done((bf16[256,128]{1,0:T(8,128)(2,1)S(1)}, bf16[256,128]{1,0:T(8,128)(2,1)}, u32[]{:S(2)}) %copy-start.4) | copy-done | bytes 65560
  6.9 0.0 copy-start.5
  6.9 0.7 %copy-done.5 = f32[20,256]{1,0:T(8,128)S(1)} copy-done((f32[20,256]{1,0:T(8,128)S(1)}, f32[20,256]{1,0:T(8,128)}, u32[]{:S(2)}) %copy-start.5) | copy-done | bytes 20504
  7.6 37.0 %shard_map.103 = (bf16[256,1280]{1,0:T(8,128)(2,1)S(1)}, f32[256,128]{1,0:T(8,128)S(1)}, f32[8,128]{1,0:T(8,128)S(1)}) custom-call(bf16[256,1280]{1,0:T(8,128)(2,1)S(1)} %copy-done, bf16[256,1280]{1,0:T(8,128)(2,1)S(1)} %copy-done.1, f32[20,256]{1,0:T(8,128)S(1)} %copy-done.5, f32[20]{0:T(128)S(1)} %copy-done.6, bf16[256,128]{1,0:T(8,128)(2,1)S(1)} %copy-done.3, ...), custom_call_target="tpu_custom_call" | custom-call | tf_op jit(solution)/shard_map/pallas_call | solution.py:407
  44.6 0.5 %slice_bitcast_fusion = f32[20]{0:T(128)} fusion(f32[8,128]{1,0:T(8,128)S(1)} %get-tuple-element.8), kind=kLoop, calls=%fused_computation | loop fusion | bytes 160 | tf_op jit(solution)/shard_map/squeeze | solution.py:452
  45.1 0.8 %copy.14 = bf16[256,1280]{1,0:T(8,128)(2,1)} copy(bf16[256,1280]{1,0:T(8,128)(2,1)S(1)} %get-tuple-element.12) | data formatting | bytes 1310720
  46.0 0.7 %copy.15 = f32[256,128]{1,0:T(8,128)} copy(f32[256,128]{1,0:T(8,128)S(1)} %get-tuple-element.13) | data formatting | bytes 262144
Async XLA Ops:
  1.3 0.7 %copy-start.6 = (f32[20]{0:T(128)S(1)}, f32[20]{0:T(128)}, u32[]{:S(2)}) copy-start(f32[20]{0:T(128)} %dec_in.1) | copy-start | bytes 244
  1.9 1.1 %copy-start = (bf16[256,1280]{1,0:T(8,128)(2,1)S(1)}, bf16[256,1280]{1,0:T(8,128)(2,1)}, u32[]{:S(2)}) copy-start(bf16[256,1280]{1,0:T(8,128)(2,1)} %x_in.1) | copy-start | bytes 1966084
  3.0 1.1 %copy-start.1 = (bf16[256,1280]{1,0:T(8,128)(2,1)S(1)}, bf16[256,1280]{1,0:T(8,128)(2,1)}, u32[]{:S(2)}) copy-start(bf16[256,1280]{1,0:T(8,128)(2,1)} %g_in.1) | copy-start | bytes 1966084
  4.1 1.1 %copy-start.2 = (f32[1,20,64,128]{3,2,1,0:T(8,128)S(1)}, f32[1,20,64,128]{3,2,1,0:T(8,128)}, u32[]{:S(2)}) copy-start(f32[1,20,64,128]{3,2,1,0:T(8,128)} %param.14) | copy-start | bytes 1966084
  5.2 0.8 %copy-start.3 = (bf16[256,128]{1,0:T(8,128)(2,1)S(1)}, bf16[256,128]{1,0:T(8,128)(2,1)}, u32[]{:S(2)}) copy-start(bf16[256,128]{1,0:T(8,128)(2,1)} %b_in.1) | copy-start | bytes 196612
  6.0 0.8 %copy-start.4 = (bf16[256,128]{1,0:T(8,128)(2,1)S(1)}, bf16[256,128]{1,0:T(8,128)(2,1)}, u32[]{:S(2)}) copy-start(bf16[256,128]{1,0:T(8,128)(2,1)} %c_in.1) | copy-start | bytes 196612
  6.9 0.7 %copy-start.5 = (f32[20,256]{1,0:T(8,128)S(1)}, f32[20,256]{1,0:T(8,128)}, u32[]{:S(2)}) copy-start(f32[20,256]{1,0:T(8,128)} %dt_in.1) | copy-start | bytes 61444

commit v3 on v2

--- a/solution.py
+++ b/solution.py
@@ -404,6 +404,11 @@
     vmem = pl.BlockSpec(memory_space=pltpu.VMEM)
     hbm = pl.BlockSpec(memory_space=pltpu.HBM)
     sem = pltpu.SemaphoreType.DMA
+    state = span_states.reshape(span_states.shape[1:])
+    operands = [
+        pltpu.with_memory_space_constraint(operand, pltpu.HBM)
+        for operand in (inputs, output_grad, time_step, decay_rate, input_map, output_map, state)
+    ]
     grad_inputs, grad_map, rates = pl.pallas_call(
         functools.partial(kernel, n, nh, width),
         out_shape=(
@@ -448,7 +453,7 @@
         compiler_params=pltpu.CompilerParams(
             collective_id=0, has_side_effects=True, vmem_limit_bytes=40 * 2**20
         ),
-    )(inputs, output_grad, time_step, decay_rate, input_map, output_map, span_states.reshape(span_states.shape[1:]), resets)
+    )(*operands, resets)
     return grad_inputs, grad_map, rates[0, :head_count]
 
 

time: 47.1 us -> 39.7 us (0.84)
  local copies, waits for them, and re-layouts: 8.33 us -> 2 us
  Pallas kernels: 37 us -> 36.2 us
    unnamed x16 -> x2, local copies, waits for them, and re-layouts: 7.81 us -> 1.49 us
    pallas_call x1, Pallas kernels: 37 us -> 36.2 us  [body(): pl.pallas_call(functools.partial(kernel, n, nh, width), out_shape=(jax.Sh...]
where the time goes in v3:
time: 39.7 us; the launch traced here: 39.5 us
  Pallas kernels  36.2 us (91%)
  local copies, waits for them, and re-layouts  2 us (5%)
  between operations  1.29 us (3%)
    pallas_call x1, Pallas kernels, body(): pl.pallas_call(functools.partial(kernel, n, nh, width), out_shape=(jax.Sh...  36.2 us
    unnamed x2, local copies, waits for them, and re-layouts  1.49 us

profile of v3, /device:TPU:0, one launch (start us, length us, event | category | flops | bytes accessed | tf_op | source)
XLA Modules:
  0.0 39.5 jit_solution(2794157069841602108)
XLA Ops:
  1.3 36.2 %shard_map.103 = (bf16[256,1280]{1,0:T(8,128)(2,1)S(1)}, f32[256,128]{1,0:T(8,128)S(1)}, f32[8,128]{1,0:T(8,128)S(1)}) custom-call(bf16[256,1280]{1,0:T(8,128)(2,1)} %x_in.1, bf16[256,1280]{1,0:T(8,128)(2,1)} %g_in.1, f32[20,256]{1,0:T(8,128)} %dt_in.1, f32[20]{0:T(128)} %dec_in.1, bf16[256,128]{1,0:T(8,128)(2,1)} %b_in.1, bf16[256,128]{1,0:T(8,128)(2,1)} %c_in.1, ...), custom_call_target="tpu_custom_call" | custom-call | tf_op jit(solution)/shard_map/pallas_call | solution.py:412
  37.5 0.5 %slice_bitcast_fusion = f32[20]{0:T(128)} fusion(f32[8,128]{1,0:T(8,128)S(1)} %get-tuple-element.8), kind=kLoop, calls=%fused_computation | loop fusion | bytes 160 | tf_op jit(solution)/shard_map/squeeze | solution.py:457
  38.0 0.8 %copy.14 = bf16[256,1280]{1,0:T(8,128)(2,1)} copy(bf16[256,1280]{1,0:T(8,128)(2,1)S(1)} %get-tuple-element.12) | data formatting | bytes 1310720
  38.9 0.7 %copy.15 = f32[256,128]{1,0:T(8,128)} copy(f32[256,128]{1,0:T(8,128)S(1)} %get-tuple-element.13) | data formatting | bytes 262144
